TPU v7x, 32 devices: a whole 2x2x4 slice. The times are simulated.
32 devices in a mesh: row: 4 (over z), col: 2 (over x), depth: 4 (over y, core).
Axes of the slice: x: 2, y: 2, z: 4, core: 2. Of those that a mesh axis runs over, the one named last changes fastest.
Arguments:
- eri_tiles: bfloat16 [48, 64, 128, 128], P('row', ('col', 'depth')), may hold values from -0.0625 to 0.0625
- screen: int32 [48, 64], P('row', ('col', 'depth')), may hold values from 0 to 1, as said below
- density_bra: bfloat16 [6144, 256], P('row', 'col'), may hold values from -6 to 6
- density_ket: bfloat16 [8192, 256], P(('col', 'depth'), 'row'), may hold values from -6 to 6
Outputs:
- coulomb_bra: float32 [6144, 256], P('row', 'col')
- coulomb_ket: float32 [8192, 256], P(('col', 'depth'), 'row')
Inputs may be any that keep to these rules, and one draw needn't show every extreme that they name: `screen`: in each device's block of 12 x 8 tiles (aligned blocks), between 16 and 64 tiles are significant; some block has exactly 64.
All inputs are finite; a program needn't handle non-finite values.
Results may differ from a plain program's by a relative error of at most 0.005.
Values may be sent and summed in bfloat16 or wider, within the bound.
A program may use at most 64 MiB of HBM per device.

v0:
```python
import jax
import jax.numpy as jnp
from jax import lax
from jax.sharding import PartitionSpec as P


def body(eri_tiles, screen, density_bra, density_ket):
    blocks_a = eri_tiles.shape[0]
    blocks_b = eri_tiles.shape[1]
    pair_size = eri_tiles.shape[2]
    masked = jnp.where(screen[:, :, None, None] > 0, eri_tiles, jnp.zeros((), jnp.bfloat16))
    fragment = lax.all_gather(density_ket, "row", axis=1, tiled=True)
    columns = fragment.shape[1]
    shaped = fragment.reshape(blocks_b, pair_size, columns)
    summed = jnp.einsum("abij,bjc->aic", masked, shaped, preferred_element_type=jnp.float32)
    bra_part = summed.reshape(blocks_a * pair_size, columns)
    fragment = lax.all_gather(density_bra, "col", axis=1, tiled=True)
    columns = fragment.shape[1]
    shaped = fragment.reshape(blocks_a, pair_size, columns)
    summed = jnp.einsum("abij,aic->bjc", masked, shaped, preferred_element_type=jnp.float32)
    ket_part = summed.reshape(blocks_b * pair_size, columns)
    coulomb_ket = lax.psum_scatter(ket_part, "row", scatter_dimension=1, tiled=True)
    shares = lax.psum_scatter(bra_part, ("col", "depth"), scatter_dimension=1, tiled=True)
    coulomb_bra = lax.all_gather(shares, "depth", axis=1, tiled=True)
    return (coulomb_bra, coulomb_ket)


def solution(mesh):
    return jax.shard_map(
        body,
        mesh=mesh,
        in_specs=(
            P("row", ("col", "depth"), None, None),
            P("row", ("col", "depth")),
            P("row", "col"),
            P(("col", "depth"), "row"),
        ),
        out_specs=(P("row", "col"), P(("col", "depth"), "row")),
        check_vma=False,
    )
```

profile of v0, /device:TPU:0, one launch (start us, length us, event | category | flops | bytes accessed | tf_op | source)
XLA Modules:
  0.0 110.0 jit_solution(13198454468047973726)
XLA Ops:
  7.2 0.0 reduce-scatter.3.cloned.1.call-start
  7.2 0.7 broadcast_compare_fusion
  7.9 0.1 copy.16
  8.0 17.6 %all_gather.9 = bf16[1024,256]{0,1:T(8,128)(2,1)S(1)} all-gather(bf16[1024,64]{0,1:T(8,128)(2,1)} %param.7), channel_id=1, replica_groups=mesh['row'=4,'col'=2,'depth'=4] {'row'}, dimensions={1}, use_global_device_ids=true | all-gather | bytes 655360 | tf_op jit(solution)/shard_map/all_gather | solution.py:12
  25.6 1.0 copy.18
  26.6 0.0 copy-start.1
  26.6 4.0 %copy_select_fusion = bf16[12,8,128,128]{3,1,2,0:T(8,128)(2,1)S(1)} fusion(bf16[12,8,128,128]{3,2,1,0:T(8,128)(2,1)} %param.4, pred[12,8]{1,0:T(8,128)(4,1)S(1)} %copy.16), kind=kLoop, calls=%fused_computation.2 | loop fusion | flops 1572864 | bytes 6291552 | tf_op jit(solution)/shard_map/jit(_where)/select_n | solution.py:11
  30.5 0.0 copy-done.1
  30.6 0.0 copy-start
  30.6 2.2 %fusion.2 = f32[1536,256]{0,1:T(8,128)} fusion(bf16[8,128,256]{2,1,0:T(8,128)(2,1)S(1)} %bitcast.18, bf16[1536,8,128]{2,1,0:T(8,128)(2,1)S(1)} %bitcast.16), kind=kOutput, calls=%fused_computation.3 | convolution fusion | flops 805306368 | bytes 5242880 | tf_op jit(solution)/shard_map/abij,bjc->aic/dot_general | solution.py:15
  32.7 0.0 reduce-scatter.3.cloned.1.call-update
  32.8 0.0 reduce-scatter.5.cloned.1.call-start
  32.8 0.0 copy-done
  32.8 3.7 %fusion.8 = bf16[8,128,12,128]{1,0,3,2:T(8,128)(2,1)} fusion(bf16[12,8,128,128]{3,2,1,0:T(8,128)(2,1)S(1)} %copy-done, pred[12,8]{1,0:T(8,128)(4,1)S(1)} %copy.16), kind=kLoop, calls=%fused_computation.6 | loop fusion | flops 1572864 | bytes 6291552 | tf_op jit(solution)/shard_map/abij,aic->bjc/dot_general | solution.py:20
  36.5 0.0 copy-start.2
  36.5 3.8 %copy.21 = bf16[8,128,12,128]{3,1,0,2:T(8,128)(2,1)S(1)} copy(bf16[8,128,12,128]{1,0,3,2:T(8,128)(2,1)} %fusion.8) | data formatting | bytes 6291456 | tf_op jit(solution)/shard_map/abij,aic->bjc/dot_general | solution.py:20
  40.3 0.0 copy-done.2
  40.3 10.2 %all_gather.11 = bf16[1536,256]{1,0:T(8,128)(2,1)S(1)} all-gather(bf16[1536,128]{1,0:T(8,128)(2,1)S(1)} %copy-done.2), channel_id=1, replica_groups=mesh['row'=4,'col'=2,'depth'=4] {'col'}, dimensions={1}, use_global_device_ids=true | all-gather | bytes 1179648 | tf_op jit(solution)/shard_map/all_gather | solution.py:17
  50.5 2.0 %convolution_bitcast_fusion = f32[1024,256]{0,1:T(8,128)} fusion(bf16[1024,12,128]{2,0,1:T(8,128)(2,1)S(1)} %bitcast.15, bf16[12,128,256]{2,1,0:T(8,128)(2,1)S(1)} %bitcast.17), kind=kOutput, calls=%fused_computation.4 | convolution fusion | flops 805306368 | bytes 4980736 | tf_op jit(solution)/shard_map/abij,aic->bjc/dot_general | solution.py:20
  52.5 0.0 reduce-scatter.5.cloned.1.call-update
  52.5 20.5 %reduce-scatter.3.cloned.1.call-done = f32[1536,32]{0,1:T(8,128)} async-done(((f32[1536,256]{0,1:T(8,128)}), f32[1536,32]{0,1:T(8,128)}) %reduce-scatter.3.cloned.1.call-update) | async-done | bytes 196624 | tf_op jit(solution)/shard_map/reduce_scatter | solution.py:23
  73.0 8.8 %all_gather.10 = f32[1536,128]{0,1:T(8,128)S(1)} all-gather(f32[1536,32]{0,1:T(8,128)} %reduce-scatter.3.cloned.1.call-done), channel_id=1, replica_groups=mesh['row'=4,'col'=2,'depth'=4] {'depth'}, dimensions={1}, use_global_device_ids=true | all-gather | bytes 983040 | tf_op jit(solution)/shard_map/all_gather | solution.py:24
  81.8 1.1 %copy.23 = f32[1536,128]{1,0:T(8,128)} copy(f32[1536,128]{0,1:T(8,128)S(1)} %all_gather.10) | data formatting | bytes 1572864
  82.9 20.3 %reduce-scatter.5.cloned.1.call-done = f32[1024,64]{0,1:T(8,128)} async-done(((f32[1024,256]{0,1:T(8,128)}), f32[1024,64]{0,1:T(8,128)}) %reduce-scatter.5.cloned.1.call-update) | async-done | bytes 262160 | tf_op jit(solution)/shard_map/reduce_scatter | solution.py:22
Async XLA Ops:
  7.2 65.8 %reduce-scatter.3.cloned.1.call-start = ((), (), s32[]{:S(2)}) async-start(), calls=%async_computation.2 | async-start | bytes 1769472 | tf_op jit(solution)/shard_map/reduce_scatter | solution.py:23
  26.6 4.0 %copy-start.1 = (bf16[1024,256]{1,0:T(8,128)(2,1)S(1)}, bf16[1024,256]{1,0:T(8,128)(2,1)}, u32[]{:S(2)}) copy-start(bf16[1024,256]{1,0:T(8,128)(2,1)} %copy.18) | copy-start | bytes 1572868
  30.6 2.3 %copy-start = (bf16[12,8,128,128]{3,2,1,0:T(8,128)(2,1)S(1)}, bf16[12,8,128,128]{3,2,1,0:T(8,128)(2,1)}, u32[]{:S(2)}) copy-start(bf16[12,8,128,128]{3,2,1,0:T(8,128)(2,1)} %param.4) | copy-start | bytes 9437188
  32.8 70.4 %reduce-scatter.5.cloned.1.call-start = ((), (), s32[]{:S(2)}) async-start(), calls=%async_computation.3 | async-start | bytes 1310720 | tf_op jit(solution)/shard_map/reduce_scatter | solution.py:22
  36.5 3.8 %copy-start.2 = (bf16[1536,128]{1,0:T(8,128)(2,1)S(1)}, bf16[1536,128]{1,0:T(8,128)(2,1)}, u32[]{:S(2)}) copy-start(bf16[1536,128]{1,0:T(8,128)(2,1)} %param.6) | copy-start | bytes 1179652
Sparse Core Ops, SparseCore 0:
  32.9 40.0 reduce-scatter.2
  75.9 27.2 reduce-scatter.4
where the time goes:
time: 110 us
  waiting for transfers between devices  40.8 us (37%)
  blocking collectives  36.5 us (33%)
  between operations  14.1 us (13%)
  other arithmetic  8.33 us (8%)
  local copies, waits for them, and re-layouts  6.08 us (6%)
  matrix products  4.18 us (4%)
    reduce_scatter x1, waiting for transfers between devices, body(): lax.psum_scatter(bra_part, ('col', 'depth'), scatter_dimension=1, tiled=T...  20.5 us
    reduce_scatter x1, waiting for transfers between devices, body(): lax.psum_scatter(ket_part, 'row', scatter_dimension=1, tiled=True)  20.3 us
    all_gather x1, blocking collectives, body(): fragment = lax.all_gather(density_ket, 'row', axis=1, tiled=True)  17.6 us
    all_gather x1, blocking collectives, body(): fragment = lax.all_gather(density_bra, 'col', axis=1, tiled=True)  10.2 us
    all_gather x1, blocking collectives, body(): coulomb_bra = lax.all_gather(shares, 'depth', axis=1, tiled=True)  8.77 us
    select_n x1, other arithmetic, body(): jnp.where(screen[:, :, None, None] > 0, eri_tiles, jnp.zeros((), jnp.bflo...  3.97 us
    dot_general x1, local copies, waits for them, and re-layouts, body(): jnp.einsum('abij,aic->bjc', masked, shaped, preferred_element_type=jnp.fl...  3.82 us
    dot_general x1, other arithmetic, body(): jnp.einsum('abij,aic->bjc', masked, shaped, preferred_element_type=jnp.fl...  3.67 us
  transfers between devices with their start and end apart: 2, of which 2 were waited for; matrix products, arithmetic and copies ran while one was open for 10% of the time, Pallas kernels for 0%

commit v1 on v0

v1 whole, which is shorter than its diff:
```python
import functools

import jax
import jax.numpy as jnp
from jax import lax
from jax.experimental import pallas as pl
from jax.experimental.pallas import tpu as pltpu
from jax.sharding import PartitionSpec as P

MESH = pl.DeviceIdType.MESH
F32 = jnp.float32


def kernel(
    sizes, eri, scr, dbra, dket, out_b, out_k,
    traw, tmat, kbuf, bbuf, kpart, down_rx, up_rx, bp, d1_rx, x_rx, y_rx, fin,
    local_sem, ks_send, ks_recv, b_send, b_recv, kr_send, kr_recv, bp_send, bp_recv,
):
    R, C, Dp = sizes
    per = R // C
    G = Dp // 2
    r, c, d = lax.axis_index("row"), lax.axis_index("col"), lax.axis_index("depth")
    h = d % 2
    g = d // 2
    sib = {"depth": d + 1 - 2 * h}
    up, down = {"row": r + 1}, {"row": r - 1}
    A, B, PS = eri.shape[0], eri.shape[1], eri.shape[2]
    rows, cols = tmat.shape
    dk = kbuf.shape[1]
    db = bbuf.shape[3]
    pending = []

    def send(src, dst, ssem, rsem, dev, cond=None):
        def make():
            return pltpu.make_async_remote_copy(
                src_ref=src, dst_ref=dst, send_sem=ssem, recv_sem=rsem,
                device_id=dev, device_id_type=MESH)

        def start():
            make().start()

        if cond is None:
            start()
        else:
            pl.when(cond)(start)
        pending.append((cond, lambda: make().wait_send()))

    def recv(dst, ssem, rsem, cond=None):
        def go():
            pltpu.make_async_remote_copy(
                src_ref=dst, dst_ref=dst, send_sem=ssem, recv_sem=rsem,
                device_id=sib, device_id_type=MESH).wait_recv()
        if cond is None:
            go()
        else:
            pl.when(cond)(go)

    half = rows // 2
    loads = [
        pltpu.make_async_copy(dket, kbuf.at[r], local_sem.at[0]),
        pltpu.make_async_copy(dbra.at[pl.ds(0, half)], bbuf.at[c, 0], local_sem.at[1]),
        pltpu.make_async_copy(dbra.at[pl.ds(half, half)], bbuf.at[c, 1], local_sem.at[2]),
        pltpu.make_async_copy(eri, traw, local_sem.at[3]),
    ]
    for one in loads:
        one.start()

    bar = pltpu.get_barrier_semaphore()

    def hello(dev):
        pl.semaphore_signal(bar, inc=1, device_id=dev, device_id_type=MESH)

    pl.when(r > 0)(lambda: hello(down))
    pl.when(r < R - 1)(lambda: hello(up))
    for o in range(1, C):
        hello({"col": (c + o) % C})
    hello(sib)
    for o in range(1, G):
        hello({"depth": (d + 2 * o) % Dp})
    peers = C + G - 1 + jnp.where(r > 0, 1, 0) + jnp.where(r < R - 1, 1, 0)
    pl.semaphore_wait(bar, peers)

    loads[0].wait()
    send(kbuf.at[r], kbuf.at[r], ks_send.at[r, 0], ks_recv.at[r], down, r > 0)
    send(kbuf.at[r], kbuf.at[r], ks_send.at[r, 1], ks_recv.at[r], up, r < R - 1)
    loads[1].wait()
    loads[2].wait()
    for o in range(1, C):
        send(bbuf.at[c, h], bbuf.at[c, h], b_send.at[o], b_recv.at[0, c], {"col": (c + o) % C})
    loads[3].wait()

    for a in range(A):
        for b in range(B):
            keep = scr[b, a] > 0
            tile = traw[a, b]
            tmat[a * PS:(a + 1) * PS, b * PS:(b + 1) * PS] = jnp.where(keep, tile, jnp.zeros_like(tile))

    def ket_block(cb):
        x = bbuf[cb].reshape(rows, db)
        res = lax.dot_general(x, tmat[...], (((0,), (0,)), ((), ())), preferred_element_type=F32)
        for j in range(per):
            kpart[cb * per + j] = res[j * dk:(j + 1) * dk]

    def ket_ends(cb):
        for j in range(per):
            t = cb * per + j
            send(kpart.at[t], down_rx.at[t], kr_send.at[0, t], kr_recv.at[0, t], down,
                 (r == R - 1) & (t < r))
        for j in reversed(range(per)):
            t = cb * per + j
            send(kpart.at[t], up_rx.at[t], kr_send.at[1, t], kr_recv.at[1, t], up,
                 (r == 0) & (t > r))

    def ket_forward(k):
        def go_down():
            recv(down_rx.at[k], kr_send.at[0, k], kr_recv.at[0, k])
            kpart[k] = kpart[k] + down_rx[k]
        cond = (r < R - 1) & (k < r)
        pl.when(cond)(go_down)
        send(kpart.at[k], down_rx.at[k], kr_send.at[0, k], kr_recv.at[0, k], down, cond)
        t = R - 1 - k

        def go_up():
            recv(up_rx.at[t], kr_send.at[1, t], kr_recv.at[1, t])
            kpart[t] = kpart[t] + up_rx[t]
        cond = (r > 0) & (t > r)
        pl.when(cond)(go_up)
        send(kpart.at[t], up_rx.at[t], kr_send.at[1, t], kr_recv.at[1, t], up, cond)

    def ket_final():
        out_k[...] = kpart[r]

        def from_up():
            recv(down_rx.at[r], kr_send.at[0, r], kr_recv.at[0, r])
            out_k[...] += down_rx[r]

        def from_down():
            recv(up_rx.at[r], kr_send.at[1, r], kr_recv.at[1, r])
            out_k[...] += up_rx[r]
        pl.when(r < R - 1)(from_up)
        pl.when(r > 0)(from_down)

    near = jnp.minimum(r, R - 1 - r)

    def slot(i):
        k = (i + 1) // 2
        inner = r - k if i % 2 == 1 else r + k
        outer = jnp.where(r > R - 1 - r, r - (i - near), r + (i - near))
        return jnp.where(i <= 2 * near, inner, outer)

    order = [slot(i) for i in range(R)]

    def bra_a(i):
        s = order[i]
        if i > 0:
            recv(kbuf.at[s], ks_send.at[s, 0], ks_recv.at[s])
            send(kbuf.at[s], kbuf.at[s], ks_send.at[s, 0], ks_recv.at[s], down, (s > r) & (r > 0))
            send(kbuf.at[s], kbuf.at[s], ks_send.at[s, 1], ks_recv.at[s], up, (s < r) & (r < R - 1))

    def bra_dot(i):
        s = order[i]
        res = lax.dot_general(kbuf[s], tmat[...], (((1,), (1,)), ((), ())), preferred_element_type=F32)
        bp[s, 0] = res[:, :half]
        bp[s, 1] = res[:, half:]
        send(bp.at[s, 1 - h], d1_rx.at[s], bp_send.at[0, s], bp_recv.at[0, s], sib)

    def bra_b(i):
        s = order[i]
        cs, j = s // per, s % per
        recv(d1_rx.at[s], bp_send.at[0, s], bp_recv.at[0, s])
        bp[s, h] = bp[s, h] + d1_rx[s]
        send(bp.at[s, h], x_rx.at[c, j], bp_send.at[1, s], bp_recv.at[1, c * per + j], {"col": cs}, cs != c)

    def bra_c(i):
        s = order[i]
        cs, j = s // per, s % per

        def go():
            total = bp[s, h]
            for o in range(1, C):
                p = (c + o) % C
                recv(x_rx.at[p, j], bp_send.at[1, s], bp_recv.at[1, p * per + j])
                total = total + x_rx[p, j]
            y_rx[j, g] = total
        pl.when(cs == c)(go)
        for o in range(1, G):
            send(y_rx.at[j, g], y_rx.at[j, g], bp_send.at[1 + o, s], bp_recv.at[2, j * G + g],
                 {"depth": (d + 2 * o) % Dp}, cs == c)

    def bra_d(i):
        s = order[i]
        cs, j = s // per, s % per

        def go():
            for o in range(1, G):
                q = (g + o) % G
                recv(y_rx.at[j, q], bp_send.at[2, s], bp_recv.at[2, j * G + q])
            total = y_rx[j, 0]
            for q in range(1, G):
                total = total + y_rx[j, q]
            fin[j, h] = total
        pl.when(cs == c)(go)
        send(fin.at[j, h], fin.at[j, h], bp_send.at[G + 1, s], bp_recv.at[3, j], sib, cs == c)

    def bra_e():
        for j in range(per):
            recv(fin.at[j, 1 - h], bp_send.at[G + 1, 0], bp_recv.at[3, j])
            out_b[j * dk:(j + 1) * dk, :half] = fin[j, 0]
            out_b[j * dk:(j + 1) * dk, half:] = fin[j, 1]

    ket_block(c)
    ket_ends(c)
    bra_dot(0)
    others = [(c + o) % C for o in range(1, C)]
    bra_a(1)
    for p in others:
        recv(bbuf.at[p, h], b_send.at[0], b_recv.at[0, p])
        send(bbuf.at[p, h], bbuf.at[p, h], b_send.at[C + p], b_recv.at[1, p], sib)
    bra_b(0)
    bra_dot(1)
    for i in range(2, R):
        bra_a(i)
        if i == 2:
            for p in others:
                recv(bbuf.at[p, 1 - h], b_send.at[0], b_recv.at[1, p])
                ket_block(p)
                ket_ends(p)
        bra_b(i - 1)
        bra_dot(i)
        if i == 2:
            bra_c(0)
            ket_forward(0)
    bra_b(R - 1)
    for i in range(1, R):
        if i < R - 1:
            ket_forward(i)
        bra_c(i)
        bra_d(i - 1)
    bra_d(R - 1)
    bra_e()
    ket_final()

    for cond, wait in pending:
        if cond is None:
            wait()
        else:
            pl.when(cond)(wait)


def body(sizes, eri_tiles, screen, density_bra, density_ket):
    R, C, Dp = sizes
    A, B, PS, _ = eri_tiles.shape
    rows, cols = A * PS, B * PS
    db, dk = density_bra.shape[1], density_ket.shape[1]
    per, G, half = R // C, Dp // 2, rows // 2
    DMA = pltpu.SemaphoreType.DMA
    anyspec = pl.BlockSpec(memory_space=pl.ANY)
    vm = pl.BlockSpec(memory_space=pltpu.VMEM)
    out_b, out_k = pl.pallas_call(
        functools.partial(kernel, sizes),
        out_shape=(jax.ShapeDtypeStruct((db, rows), F32), jax.ShapeDtypeStruct((dk, cols), F32)),
        in_specs=[anyspec, pl.BlockSpec(memory_space=pltpu.SMEM), anyspec, anyspec],
        out_specs=(vm, vm),
        scratch_shapes=[
            pltpu.VMEM((A, B, PS, PS), jnp.bfloat16),
            pltpu.VMEM((rows, cols), jnp.bfloat16),
            pltpu.VMEM((R, dk, cols), jnp.bfloat16),
            pltpu.VMEM((C, 2, half, db), jnp.bfloat16),
            pltpu.VMEM((R, dk, cols), F32),
            pltpu.VMEM((R, dk, cols), F32),
            pltpu.VMEM((R, dk, cols), F32),
            pltpu.VMEM((R, 2, dk, half), F32),
            pltpu.VMEM((R, dk, half), F32),
            pltpu.VMEM((C, per, dk, half), F32),
            pltpu.VMEM((per, G, dk, half), F32),
            pltpu.VMEM((per, 2, dk, half), F32),
            DMA((4,)),
            DMA((R, 2)), DMA((R,)),
            DMA((2 * C,)), DMA((2, C)),
            DMA((2, R)), DMA((2, R)),
            DMA((G + 2, R)), DMA((4, max(R, per * G))),
        ],
        compiler_params=pltpu.CompilerParams(
            collective_id=0, has_side_effects=True, vmem_limit_bytes=56 * 1024 * 1024),
    )(eri_tiles, screen.T, density_bra, density_ket.T)
    return out_b.T, out_k.T


def solution(mesh):
    sizes = (mesh.shape["row"], mesh.shape["col"], mesh.shape["depth"])
    return jax.shard_map(
        functools.partial(body, sizes),
        mesh=mesh,
        in_specs=(
            P("row", ("col", "depth"), None, None),
            P("row", ("col", "depth")),
            P("row", "col"),
            P(("col", "depth"), "row"),
        ),
        out_specs=(P("row", "col"), P(("col", "depth"), "row")),
        check_vma=False,
    )
```

time: 110 us -> 61.8 us (0.56)
  the two profiles are of different devices: /device:TPU:0 before, /device:TPU:29 now
where the time goes in v1:
time: 61.8 us; the launch traced here: 61.6 us
  Pallas kernels  57 us (92%)
  local copies, waits for them, and re-layouts  3.95 us (6%)
  between operations  0.64 us (1%)
    pallas_call x1, Pallas kernels, body(): pl.pallas_call(functools.partial(kernel, sizes), out_shape=(jax.ShapeDtyp...  57 us
    unnamed x2, local copies, waits for them, and re-layouts  3.95 us

profile of v1, /device:TPU:29, one launch (start us, length us, event | category | flops | bytes accessed | tf_op | source)
XLA Modules:
  0.0 61.6 jit_solution(15000298554700815093)
XLA Ops:
  0.6 57.0 %shard_map.59 = (f32[128,1536]{1,0:T(8,128)}, f32[64,1024]{1,0:T(8,128)}) custom-call(bf16[12,8,128,128]{3,2,1,0:T(8,128)(2,1)} %eri.1, s32[8,12]{1,0:T(8,128)} %bitcast.7, bf16[1536,128]{1,0:T(8,128)(2,1)} %dbra.1, bf16[64,1024]{1,0:T(8,128)(2,1)} %bitcast.6), custom_call_target="tpu_custom_call" | custom-call | tf_op jit(solution)/shard_map/pallas_call | solution.py:259
  57.6 2.3 %copy.6 = f32[1536,128]{1,0:T(8,128)} copy(f32[1536,128]{0,1:T(8,128)} %bitcast.4) | data formatting | bytes 1572864
  59.9 1.7 %copy.8 = f32[1024,64]{0,1:T(8,128)} copy(f32[1024,64]{0,1:T(8,128)} %bitcast.5) | data formatting | bytes 524288

commit v2 on v1

--- a/solution.py
+++ b/solution.py
@@ -13,7 +13,7 @@
 
 def kernel(
     sizes, eri, scr, dbra, dket, out_b, out_k,
-    traw, tmat, kbuf, bbuf, kpart, down_rx, up_rx, bp, d1_rx, x_rx, y_rx, fin,
+    traw, tmat, kbuf, bbuf, kpart, k_rx, bp, d1_rx, x_rx, y_rx, fin,
     local_sem, ks_send, ks_recv, b_send, b_recv, kr_send, kr_recv, bp_send, bp_recv,
 ):
     R, C, Dp = sizes
@@ -26,7 +26,9 @@
     up, down = {"row": r + 1}, {"row": r - 1}
     A, B, PS = eri.shape[0], eri.shape[1], eri.shape[2]
     rows, cols = tmat.shape
-    dk = kbuf.shape[1]
+    dk = kbuf.shape[2]
+    H = kbuf.shape[1]
+    part = cols // H
     db = bbuf.shape[3]
     pending = []
 
@@ -57,11 +59,16 @@
 
     half = rows // 2
     loads = [
-        pltpu.make_async_copy(dket, kbuf.at[r], local_sem.at[0]),
-        pltpu.make_async_copy(dbra.at[pl.ds(0, half)], bbuf.at[c, 0], local_sem.at[1]),
-        pltpu.make_async_copy(dbra.at[pl.ds(half, half)], bbuf.at[c, 1], local_sem.at[2]),
-        pltpu.make_async_copy(eri, traw, local_sem.at[3]),
+        pltpu.make_async_copy(dbra.at[pl.ds(0, half)], bbuf.at[c, 0], local_sem.at[0]),
+        pltpu.make_async_copy(dbra.at[pl.ds(half, half)], bbuf.at[c, 1], local_sem.at[1]),
+        pltpu.make_async_copy(eri, traw, local_sem.at[2]),
     ]
+    kloads = [
+        pltpu.make_async_copy(dket.at[:, pl.ds(u * part, part)], kbuf.at[r, u], local_sem.at[3 + u])
+        for u in range(H)
+    ]
+    for one in kloads:
+        one.start()
     for one in loads:
         one.start()
 
@@ -80,14 +87,19 @@
     peers = C + G - 1 + jnp.where(r > 0, 1, 0) + jnp.where(r < R - 1, 1, 0)
     pl.semaphore_wait(bar, peers)
 
+    def ket_send(s, u, dirn, cond):
+        send(kbuf.at[s, u], kbuf.at[s, u], ks_send.at[s, dirn, u], ks_recv.at[s, u],
+             up if dirn else down, cond)
+
+    for u in range(H):
+        kloads[u].wait()
+        ket_send(r, u, 0, r > 0)
+        ket_send(r, u, 1, r < R - 1)
     loads[0].wait()
-    send(kbuf.at[r], kbuf.at[r], ks_send.at[r, 0], ks_recv.at[r], down, r > 0)
-    send(kbuf.at[r], kbuf.at[r], ks_send.at[r, 1], ks_recv.at[r], up, r < R - 1)
     loads[1].wait()
-    loads[2].wait()
     for o in range(1, C):
         send(bbuf.at[c, h], bbuf.at[c, h], b_send.at[o], b_recv.at[0, c], {"col": (c + o) % C})
-    loads[3].wait()
+    loads[2].wait()
 
     for a in range(A):
         for b in range(B):
@@ -99,46 +111,49 @@
         x = bbuf[cb].reshape(rows, db)
         res = lax.dot_general(x, tmat[...], (((0,), (0,)), ((), ())), preferred_element_type=F32)
         for j in range(per):
-            kpart[cb * per + j] = res[j * dk:(j + 1) * dk]
+            for u in range(H):
+                kpart[cb * per + j, u] = res[j * dk:(j + 1) * dk, u * part:(u + 1) * part]
+
+    def sum_send(t, u, dirn, cond):
+        send(kpart.at[t, u], k_rx.at[dirn, t, u], kr_send.at[dirn, t, u], kr_recv.at[dirn, t, u],
+             {"row": r - 1 + 2 * dirn}, cond)
+
+    def sum_recv(t, u, dirn):
+        recv(k_rx.at[dirn, t, u], kr_send.at[dirn, t, u], kr_recv.at[dirn, t, u])
 
     def ket_ends(cb):
         for j in range(per):
             t = cb * per + j
-            send(kpart.at[t], down_rx.at[t], kr_send.at[0, t], kr_recv.at[0, t], down,
-                 (r == R - 1) & (t < r))
+            for u in range(H):
+                sum_send(t, u, 0, (r == R - 1) & (t < r))
         for j in reversed(range(per)):
             t = cb * per + j
-            send(kpart.at[t], up_rx.at[t], kr_send.at[1, t], kr_recv.at[1, t], up,
-                 (r == 0) & (t > r))
-
-    def ket_forward(k):
-        def go_down():
-            recv(down_rx.at[k], kr_send.at[0, k], kr_recv.at[0, k])
-            kpart[k] = kpart[k] + down_rx[k]
-        cond = (r < R - 1) & (k < r)
-        pl.when(cond)(go_down)
-        send(kpart.at[k], down_rx.at[k], kr_send.at[0, k], kr_recv.at[0, k], down, cond)
-        t = R - 1 - k
-
-        def go_up():
-            recv(up_rx.at[t], kr_send.at[1, t], kr_recv.at[1, t])
-            kpart[t] = kpart[t] + up_rx[t]
-        cond = (r > 0) & (t > r)
-        pl.when(cond)(go_up)
-        send(kpart.at[t], up_rx.at[t], kr_send.at[1, t], kr_recv.at[1, t], up, cond)
+            for u in range(H):
+                sum_send(t, u, 1, (r == 0) & (t > r))
+
+    first = (c * 2) // C
+
+    def ket_forward(late, k):
+        dirn = 1 - first if late else first
+        t = jnp.where(dirn == 0, k, R - 1 - k)
+        cond = jnp.where(dirn == 0, (r < R - 1) & (t < r), (r > 0) & (t > r))
+        for u in range(H):
+            def go():
+                sum_recv(t, u, dirn)
+                kpart[t, u] = kpart[t, u] + k_rx[dirn, t, u]
+            pl.when(cond)(go)
+            sum_send(t, u, dirn, cond)
 
     def ket_final():
-        out_k[...] = kpart[r]
-
-        def from_up():
-            recv(down_rx.at[r], kr_send.at[0, r], kr_recv.at[0, r])
-            out_k[...] += down_rx[r]
-
-        def from_down():
-            recv(up_rx.at[r], kr_send.at[1, r], kr_recv.at[1, r])
-            out_k[...] += up_rx[r]
-        pl.when(r < R - 1)(from_up)
-        pl.when(r > 0)(from_down)
+        for u in range(H):
+            at = slice(u * part, (u + 1) * part)
+            out_k[:, at] = kpart[r, u]
+
+            def take(dirn):
+                sum_recv(r, u, dirn)
+                out_k[:, at] += k_rx[dirn, r, u]
+            pl.when(r < R - 1)(lambda: take(0))
+            pl.when(r > 0)(lambda: take(1))
 
     near = jnp.minimum(r, R - 1 - r)
 
@@ -150,16 +165,23 @@
 
     order = [slot(i) for i in range(R)]
 
-    def bra_a(i):
-        s = order[i]
-        if i > 0:
-            recv(kbuf.at[s], ks_send.at[s, 0], ks_recv.at[s])
-            send(kbuf.at[s], kbuf.at[s], ks_send.at[s, 0], ks_recv.at[s], down, (s > r) & (r > 0))
-            send(kbuf.at[s], kbuf.at[s], ks_send.at[s, 1], ks_recv.at[s], up, (s < r) & (r < R - 1))
+    def bra_a(i, close=None):
+        s = order[i]
+        here = None if close is None else (near >= 1 if close else near < 1)
+
+        def gate(x):
+            return x if here is None else x & here
+        for u in range(H):
+            recv(kbuf.at[s, u], ks_send.at[s, 0, u], ks_recv.at[s, u], here)
+            ket_send(s, u, 0, gate((s > r) & (r > 0)))
+            ket_send(s, u, 1, gate((s < r) & (r < R - 1)))
 
     def bra_dot(i):
         s = order[i]
-        res = lax.dot_general(kbuf[s], tmat[...], (((1,), (1,)), ((), ())), preferred_element_type=F32)
+        res = sum(
+            lax.dot_general(kbuf[s, u], tmat[:, u * part:(u + 1) * part], (((1,), (1,)), ((), ())),
+                            preferred_element_type=F32)
+            for u in range(H))
         bp[s, 0] = res[:, :half]
         bp[s, 1] = res[:, half:]
         send(bp.at[s, 1 - h], d1_rx.at[s], bp_send.at[0, s], bp_recv.at[0, s], sib)
@@ -208,35 +230,50 @@
             out_b[j * dk:(j + 1) * dk, :half] = fin[j, 0]
             out_b[j * dk:(j + 1) * dk, half:] = fin[j, 1]
 
+    others = [(c + o) % C for o in range(1, C)]
     ket_block(c)
     ket_ends(c)
     bra_dot(0)
-    others = [(c + o) % C for o in range(1, C)]
     bra_a(1)
+    bra_b(0)
+    bra_dot(1)
     for p in others:
         recv(bbuf.at[p, h], b_send.at[0], b_recv.at[0, p])
         send(bbuf.at[p, h], bbuf.at[p, h], b_send.at[C + p], b_recv.at[1, p], sib)
-    bra_b(0)
-    bra_dot(1)
+    bra_a(2, True)
+    bra_b(1)
+    for p in others:
+        recv(bbuf.at[p, 1 - h], b_send.at[0], b_recv.at[1, p])
+        ket_block(p)
+        ket_ends(p)
+    bra_a(2, False)
+    bra_dot(2)
+    bra_a(3, True)
+    ket_forward(False, 0)
+    bra_c(0)
+    bra_b(2)
+    bra_a(3, False)
+    bra_dot(3)
+    ket_forward(False, 1)
+    bra_c(1)
+    bra_b(3)
+    for i in range(4, R):
+        bra_a(i)
+        bra_dot(i)
+        bra_b(i)
+    ket_forward(True, 0)
+    bra_d(0)
+    bra_c(2)
+    for k in range(2, R - 1):
+        ket_forward(False, k)
+        ket_forward(True, k - 1)
+    bra_d(1)
+    bra_c(3)
+    for i in range(4, R):
+        bra_c(i)
+    ket_forward(True, R - 2)
     for i in range(2, R):
-        bra_a(i)
-        if i == 2:
-            for p in others:
-                recv(bbuf.at[p, 1 - h], b_send.at[0], b_recv.at[1, p])
-                ket_block(p)
-                ket_ends(p)
-        bra_b(i - 1)
-        bra_dot(i)
-        if i == 2:
-            bra_c(0)
-            ket_forward(0)
-    bra_b(R - 1)
-    for i in range(1, R):
-        if i < R - 1:
-            ket_forward(i)
-        bra_c(i)
-        bra_d(i - 1)
-    bra_d(R - 1)
+        bra_d(i)
     bra_e()
     ket_final()
 
@@ -252,7 +289,7 @@
     A, B, PS, _ = eri_tiles.shape
     rows, cols = A * PS, B * PS
     db, dk = density_bra.shape[1], density_ket.shape[1]
-    per, G, half = R // C, Dp // 2, rows // 2
+    per, G, half, H = R // C, Dp // 2, rows // 2, 2
     DMA = pltpu.SemaphoreType.DMA
     anyspec = pl.BlockSpec(memory_space=pl.ANY)
     vm = pl.BlockSpec(memory_space=pltpu.VMEM)
@@ -264,24 +301,23 @@
         scratch_shapes=[
             pltpu.VMEM((A, B, PS, PS), jnp.bfloat16),
             pltpu.VMEM((rows, cols), jnp.bfloat16),
-            pltpu.VMEM((R, dk, cols), jnp.bfloat16),
+            pltpu.VMEM((R, H, dk, cols // H), jnp.bfloat16),
             pltpu.VMEM((C, 2, half, db), jnp.bfloat16),
-            pltpu.VMEM((R, dk, cols), F32),
-            pltpu.VMEM((R, dk, cols), F32),
-            pltpu.VMEM((R, dk, cols), F32),
+            pltpu.VMEM((R, H, dk, cols // H), F32),
+            pltpu.VMEM((2, R, H, dk, cols // H), F32),
             pltpu.VMEM((R, 2, dk, half), F32),
             pltpu.VMEM((R, dk, half), F32),
             pltpu.VMEM((C, per, dk, half), F32),
             pltpu.VMEM((per, G, dk, half), F32),
             pltpu.VMEM((per, 2, dk, half), F32),
-            DMA((4,)),
-            DMA((R, 2)), DMA((R,)),
+            DMA((3 + H,)),
+            DMA((R, 2, H)), DMA((R, H)),
             DMA((2 * C,)), DMA((2, C)),
-            DMA((2, R)), DMA((2, R)),
+            DMA((2, R, H)), DMA((2, R, H)),
             DMA((G + 2, R)), DMA((4, max(R, per * G))),
         ],
         compiler_params=pltpu.CompilerParams(
-            collective_id=0, has_side_effects=True, vmem_limit_bytes=56 * 1024 * 1024),
+            collective_id=0, has_side_effects=True, vmem_limit_bytes=28 * 1024 * 1024),
     )(eri_tiles, screen.T, density_bra, density_ket.T)
     return out_b.T, out_k.T
 

time: 61.8 us -> 50.8 us (0.82)
  the two profiles are of different devices: /device:TPU:29 before, /device:TPU:11 now
where the time goes in v2:
time: 50.8 us; the launch traced here: 50.5 us
  Pallas kernels  43.5 us (86%)
  local copies, waits for them, and re-layouts  6.32 us (12%)
  between operations  0.65 us (1%)
    pallas_call x1, Pallas kernels, body(): pl.pallas_call(functools.partial(kernel, sizes), out_shape=(jax.ShapeDtyp...  43.5 us
    unnamed x10, local copies, waits for them, and re-layouts  6.32 us

profile of v2, /device:TPU:11, one launch (start us, length us, event | category | flops | bytes accessed | tf_op | source)
XLA Modules:
  0.0 50.5 jit_solution(12420839933105059788)
XLA Ops:
  0.6 0.0 copy-start
  0.6 1.9 %copy-done = bf16[12,8,128,128]{3,2,1,0:T(8,128)(2,1)S(1)} copy-done((bf16[12,8,128,128]{3,2,1,0:T(8,128)(2,1)S(1)}, bf16[12,8,128,128]{3,2,1,0:T(8,128)(2,1)}, u32[]{:S(2)}) %copy-start) | copy-done | bytes 3145752
  2.5 0.0 copy-start.1
  2.5 1.0 %copy-done.1 = bf16[1536,128]{1,0:T(8,128)(2,1)S(1)} copy-done((bf16[1536,128]{1,0:T(8,128)(2,1)S(1)}, bf16[1536,128]{1,0:T(8,128)(2,1)}, u32[]{:S(2)}) %copy-start.1) | copy-done | bytes 393240
  3.5 0.0 copy-start.2
  3.5 0.9 %copy-done.2 = bf16[1024,64]{0,1:T(8,128)(2,1)S(1)} copy-done((bf16[1024,64]{0,1:T(8,128)(2,1)S(1)}, bf16[1024,64]{0,1:T(8,128)(2,1)}, u32[]{:S(2)}) %copy-start.2) | copy-done | bytes 131096
  4.4 0.0 copy-start.3
  4.4 0.7 %copy-done.3 = s32[12,8]{0,1:T(8,128)S(1)} copy-done((s32[12,8]{0,1:T(8,128)S(1)}, s32[12,8]{0,1:T(8,128)}, u32[]{:S(2)}) %copy-start.3) | copy-done | bytes 408
  5.1 43.5 %shard_map.59 = (f32[128,1536]{1,0:T(8,128)S(1)}, f32[64,1024]{1,0:T(8,128)S(1)}) custom-call(bf16[12,8,128,128]{3,2,1,0:T(8,128)(2,1)S(1)} %copy-done, s32[8,12]{1,0:T(8,128)S(1)} %bitcast.7, bf16[1536,128]{1,0:T(8,128)(2,1)S(1)} %copy-done.1, bf16[64,1024]{1,0:T(8,128)(2,1)S(1)} %bitcast.6), custom_call_target="tpu_custom_call" | custom-call | tf_op jit(solution)/shard_map/pallas_call | solution.py:296
  48.7 1.1 %copy.6 = f32[1536,128]{1,0:T(8,128)} copy(f32[1536,128]{0,1:T(8,128)S(1)} %bitcast.4) | data formatting | bytes 1572864
  49.8 0.7 %copy.8 = f32[1024,64]{0,1:T(8,128)} copy(f32[1024,64]{0,1:T(8,128)S(1)} %bitcast.5) | data formatting | bytes 524288
Async XLA Ops:
  0.6 1.9 %copy-start = (bf16[12,8,128,128]{3,2,1,0:T(8,128)(2,1)S(1)}, bf16[12,8,128,128]{3,2,1,0:T(8,128)(2,1)}, u32[]{:S(2)}) copy-start(bf16[12,8,128,128]{3,2,1,0:T(8,128)(2,1)} %eri.1) | copy-start | bytes 9437188
  2.5 1.0 %copy-start.1 = (bf16[1536,128]{1,0:T(8,128)(2,1)S(1)}, bf16[1536,128]{1,0:T(8,128)(2,1)}, u32[]{:S(2)}) copy-start(bf16[1536,128]{1,0:T(8,128)(2,1)} %dbra.1) | copy-start | bytes 1179652
  3.5 0.9 %copy-start.2 = (bf16[1024,64]{0,1:T(8,128)(2,1)S(1)}, bf16[1024,64]{0,1:T(8,128)(2,1)}, u32[]{:S(2)}) copy-start(bf16[1024,64]{0,1:T(8,128)(2,1)} %param.7) | copy-start | bytes 393220
  4.4 0.7 %copy-start.3 = (s32[12,8]{0,1:T(8,128)S(1)}, s32[12,8]{0,1:T(8,128)}, u32[]{:S(2)}) copy-start(s32[12,8]{0,1:T(8,128)} %param.5) | copy-start | bytes 1156

commit v3 on v2

--- a/solution.py
+++ b/solution.py
@@ -12,8 +12,8 @@
 
 
 def kernel(
-    sizes, eri, scr, dbra, dket, out_b, out_k,
-    traw, tmat, kbuf, bbuf, kpart, k_rx, bp, d1_rx, x_rx, y_rx, fin,
+    sizes, eri, screen, dbra, dket, out_b, out_k,
+    scr, traw, tmat, kbuf, bbuf, kpart, k_rx, bp, d1_rx, x_rx, y_rx, fin,
     local_sem, ks_send, ks_recv, b_send, b_recv, kr_send, kr_recv, bp_send, bp_recv,
 ):
     R, C, Dp = sizes
@@ -62,6 +62,7 @@
         pltpu.make_async_copy(dbra.at[pl.ds(0, half)], bbuf.at[c, 0], local_sem.at[0]),
         pltpu.make_async_copy(dbra.at[pl.ds(half, half)], bbuf.at[c, 1], local_sem.at[1]),
         pltpu.make_async_copy(eri, traw, local_sem.at[2]),
+        pltpu.make_async_copy(screen, scr, local_sem.at[3 + H]),
     ]
     kloads = [
         pltpu.make_async_copy(dket.at[:, pl.ds(u * part, part)], kbuf.at[r, u], local_sem.at[3 + u])
@@ -100,6 +101,7 @@
     for o in range(1, C):
         send(bbuf.at[c, h], bbuf.at[c, h], b_send.at[o], b_recv.at[0, c], {"col": (c + o) % C})
     loads[2].wait()
+    loads[3].wait()
 
     for a in range(A):
         for b in range(B):
@@ -291,14 +293,15 @@
     db, dk = density_bra.shape[1], density_ket.shape[1]
     per, G, half, H = R // C, Dp // 2, rows // 2, 2
     DMA = pltpu.SemaphoreType.DMA
-    anyspec = pl.BlockSpec(memory_space=pl.ANY)
+    hbm = pl.BlockSpec(memory_space=pltpu.HBM)
     vm = pl.BlockSpec(memory_space=pltpu.VMEM)
     out_b, out_k = pl.pallas_call(
         functools.partial(kernel, sizes),
         out_shape=(jax.ShapeDtypeStruct((db, rows), F32), jax.ShapeDtypeStruct((dk, cols), F32)),
-        in_specs=[anyspec, pl.BlockSpec(memory_space=pltpu.SMEM), anyspec, anyspec],
+        in_specs=[hbm, hbm, hbm, hbm],
         out_specs=(vm, vm),
         scratch_shapes=[
+            pltpu.SMEM((B, A), jnp.int32),
             pltpu.VMEM((A, B, PS, PS), jnp.bfloat16),
             pltpu.VMEM((rows, cols), jnp.bfloat16),
             pltpu.VMEM((R, H, dk, cols // H), jnp.bfloat16),
@@ -310,7 +313,7 @@
             pltpu.VMEM((C, per, dk, half), F32),
             pltpu.VMEM((per, G, dk, half), F32),
             pltpu.VMEM((per, 2, dk, half), F32),
-            DMA((3 + H,)),
+            DMA((4 + H,)),
             DMA((R, 2, H)), DMA((R, H)),
             DMA((2 * C,)), DMA((2, C)),
             DMA((2, R, H)), DMA((2, R, H)),
@@ -318,7 +321,7 @@
         ],
         compiler_params=pltpu.CompilerParams(
             collective_id=0, has_side_effects=True, vmem_limit_bytes=28 * 1024 * 1024),
-    )(eri_tiles, screen.T, density_bra, density_ket.T)
+    )(*(pltpu.with_memory_space_constraint(x, pltpu.HBM) for x in (eri_tiles, screen.T, density_bra, density_ket.T)))
     return out_b.T, out_k.T
 
 

time: 50.8 us -> 45.4 us (0.89)
  local copies, waits for them, and re-layouts: 6.32 us -> 1.85 us
  Pallas kernels: 43.5 us -> 42.8 us
    unnamed x10 -> x2, local copies, waits for them, and re-layouts: 6.32 us -> 1.85 us
    pallas_call x1, Pallas kernels: 43.5 us -> 42.8 us  [body(): pl.pallas_call(functools.partial(kernel, sizes), out_shape=(jax.ShapeDtyp...]
where the time goes in v3:
time: 45.4 us; the launch traced here: 45.3 us
  Pallas kernels  42.8 us (94%)
  local copies, waits for them, and re-layouts  1.85 us (4%)
  between operations  0.64 us (1%)
    pallas_call x1, Pallas kernels, body(): pl.pallas_call(functools.partial(kernel, sizes), out_shape=(jax.ShapeDtyp...  42.8 us
    unnamed x2, local copies, waits for them, and re-layouts  1.85 us

profile of v3, /device:TPU:11, one launch (start us, length us, event | category | flops | bytes accessed | tf_op | source)
XLA Modules:
  0.0 45.3 jit_solution(9146764356269948833)
XLA Ops:
  0.6 42.8 %shard_map.59 = (f32[128,1536]{1,0:T(8,128)S(1)}, f32[64,1024]{1,0:T(8,128)S(1)}) custom-call(bf16[12,8,128,128]{3,2,1,0:T(8,128)(2,1)} %eri.1, s32[8,12]{1,0:T(8,128)} %bitcast.7, bf16[1536,128]{1,0:T(8,128)(2,1)} %dbra.1, bf16[64,1024]{1,0:T(8,128)(2,1)} %bitcast.6), custom_call_target="tpu_custom_call" | custom-call | tf_op jit(solution)/shard_map/pallas_call | solution.py:298
  43.4 1.1 %copy.6 = f32[1536,128]{1,0:T(8,128)} copy(f32[1536,128]{0,1:T(8,128)S(1)} %bitcast.4) | data formatting | bytes 1572864
  44.6 0.7 %copy.8 = f32[1024,64]{0,1:T(8,128)} copy(f32[1024,64]{0,1:T(8,128)S(1)} %bitcast.5) | data formatting | bytes 524288

commit v4 on v3

--- a/solution.py
+++ b/solution.py
@@ -263,14 +263,14 @@
         bra_a(i)
         bra_dot(i)
         bra_b(i)
+    bra_c(2)
     ket_forward(True, 0)
+    bra_c(3)
     bra_d(0)
-    bra_c(2)
     for k in range(2, R - 1):
         ket_forward(False, k)
         ket_forward(True, k - 1)
     bra_d(1)
-    bra_c(3)
     for i in range(4, R):
         bra_c(i)
     ket_forward(True, R - 2)

time: 45.4 us -> 41.3 us (0.910)
  Pallas kernels: 42.8 us -> 38.6 us
    pallas_call x1, Pallas kernels: 42.8 us -> 38.6 us  [body(): pl.pallas_call(functools.partial(kernel, sizes), out_shape=(jax.ShapeDtyp...]
where the time goes in v4:
time: 41.3 us; the launch traced here: 41.1 us
  Pallas kernels  38.6 us (93%)
  local copies, waits for them, and re-layouts  1.85 us (4%)
  between operations  0.64 us (2%)
    pallas_call x1, Pallas kernels, body(): pl.pallas_call(functools.partial(kernel, sizes), out_shape=(jax.ShapeDtyp...  38.6 us
    unnamed x2, local copies, waits for them, and re-layouts  1.85 us

profile of v4, /device:TPU:11, one launch (start us, length us, event | category | flops | bytes accessed | tf_op | source)
XLA Modules:
  0.0 41.1 jit_solution(13825379414920572574)
XLA Ops:
  0.6 38.6 %shard_map.59 = (f32[128,1536]{1,0:T(8,128)S(1)}, f32[64,1024]{1,0:T(8,128)S(1)}) custom-call(bf16[12,8,128,128]{3,2,1,0:T(8,128)(2,1)} %eri.1, s32[8,12]{1,0:T(8,128)} %bitcast.7, bf16[1536,128]{1,0:T(8,128)(2,1)} %dbra.1, bf16[64,1024]{1,0:T(8,128)(2,1)} %bitcast.6), custom_call_target="tpu_custom_call" | custom-call | tf_op jit(solution)/shard_map/pallas_call | solution.py:298
  39.3 1.1 %copy.6 = f32[1536,128]{1,0:T(8,128)} copy(f32[1536,128]{0,1:T(8,128)S(1)} %bitcast.4) | data formatting | bytes 1572864
  40.4 0.7 %copy.8 = f32[1024,64]{0,1:T(8,128)} copy(f32[1024,64]{0,1:T(8,128)S(1)} %bitcast.5) | data formatting | bytes 524288
